TPU v7x, 32 devices: a whole 2x2x4 slice. The times are simulated.
32 devices in a mesh: ma: 16 (over z, y, core), row: 2 (over x).
Axes of the slice: x: 2, y: 2, z: 4, core: 2. Of those that a mesh axis runs over, the one named last changes fastest.
Arguments:
- spectral: bfloat16 [384, 2, 384, 2, 769], P('ma', None, 'row'), may hold values from -0.011047363 to 0.011047363
- latitude_basis: bfloat16 [384, 769, 1152], P('ma'), may hold values from -0.21875 to 0.21875
- pair_orders: int32 [384], replicated, may hold values from 0 to 383, each once
Outputs:
- grid_values: bfloat16 [64, 2, 1152, 2304], P('row', None, 'ma')
Inputs may be any that keep to these rules, and one draw needn't show every extreme that they name: A permutation of 0 to 383; slot p holds the orders pair_orders[p] and 767 - pair_orders[p].
All inputs are finite; a program needn't handle non-finite values.
Results may differ from a plain program's by a relative error of at most 0.0066.
Values may be sent and summed in bfloat16 or wider, within the bound.
No kernel may reach another device: no remote copies, remote signals or barrier semaphores. Data moves between devices by JAX's collectives and lax.ppermute only.
A program may use at most 192 MiB of HBM per device.

v0:
```python
import math

import jax
import jax.numpy as jnp
from jax import lax
from jax.sharding import PartitionSpec as P

NLON = 2304
LEV = 64


def radial_table(total_modes, levels):
    mode_index = lax.broadcasted_iota(jnp.int32, (total_modes, levels), 0)
    points = lax.broadcasted_iota(jnp.int32, (total_modes, levels), 1)
    period = 2 * (total_modes - 1)
    phase_steps = mode_index * points % period
    return jnp.cos(phase_steps.astype(jnp.float32) * (2.0 * math.pi / period)).astype(jnp.bfloat16)


def longitude_table(pair_orders, degrees, points):
    orders = jnp.stack([pair_orders, degrees - 1 - pair_orders], axis=1)
    weights = jnp.where(orders == 0, 1.0, 2.0).astype(jnp.float32)
    phase_index = orders[:, :, None] * lax.broadcasted_iota(jnp.int32, (1, 1, points), 2) % points
    angles = phase_index.astype(jnp.float32) * (2.0 * math.pi / points)
    real_part = weights[:, :, None] * jnp.cos(angles)
    imag_part = -weights[:, :, None] * jnp.sin(angles)
    stacked = jnp.stack([real_part, imag_part], axis=2)
    return stacked.reshape(-1, points).astype(jnp.bfloat16)


def order_selectors(local_orders, degrees, packed):
    packed_rows = lax.broadcasted_iota(jnp.int32, (local_orders.shape[0], packed), 1)
    below_split = packed_rows < (degrees - local_orders)[:, None]
    return jnp.stack([below_split, jnp.logical_not(below_split)], axis=1).astype(jnp.bfloat16)


def per_device(spectral, latitude_basis, pair_orders):
    pair_dev = spectral.shape[0]
    local_modes = spectral.shape[2]
    fields = spectral.shape[3]
    packed = spectral.shape[4]
    degrees = packed - 1
    row_count = lax.axis_size("row")
    total_modes = local_modes * row_count
    level_dev = LEV // row_count
    cheb_table = radial_table(total_modes, LEV)
    own_rows = lax.dynamic_slice_in_dim(
        cheb_table, lax.axis_index("row") * local_modes, local_modes, 0
    )
    scattered = lax.psum_scatter(
        jnp.einsum("pckfr,kl->lpcfr", spectral, own_rows, preferred_element_type=jnp.float32),
        "row",
        scatter_dimension=0,
        tiled=True,
    )
    summed = jnp.transpose(scattered, (1, 2, 0, 3, 4))
    levels = summed.astype(jnp.bfloat16)
    local_orders = lax.dynamic_slice_in_dim(
        pair_orders, lax.axis_index("ma") * pair_dev, pair_dev, 0
    )
    selectors = order_selectors(local_orders, degrees, packed)
    masked = levels[:, None] * selectors[:, :, None, None, None, :]
    lon_table = longitude_table(pair_orders, degrees, NLON)
    block_levels = masked.shape[3]
    fourier = jnp.einsum(
        "phclfr,prt->phclft", masked, latitude_basis, preferred_element_type=jnp.float32
    ).astype(jnp.bfloat16)
    fourier = fourier.reshape(pair_dev * 4, block_levels * fields, fourier.shape[-1])
    synthesized = jnp.einsum(
        "oit,on->itn",
        lax.all_to_all(fourier, "ma", split_axis=2, concat_axis=0, tiled=True),
        lon_table,
        preferred_element_type=jnp.float32,
    ).astype(jnp.bfloat16)
    return synthesized.reshape(level_dev, fields, synthesized.shape[1], synthesized.shape[2])


def solution(mesh):
    return jax.shard_map(
        per_device,
        mesh=mesh,
        in_specs=(P("ma", None, "row", None, None), P("ma", None, None), P()),
        out_specs=P("row", None, "ma", None),
        check_vma=False,
    )
```

profile of v0, /device:TPU:13, one launch (start us, length us, event | category | flops | bytes accessed | tf_op | source)
XLA Modules:
  0.0 924.5 jit_solution(17404826338071164951)
XLA Ops:
  6.5 0.0 reduce-scatter.2.cloned.1.call-start
  6.5 0.1 fusion.15
  6.7 25.3 %fusion.2 = f32[64,24,2,2,769]{4,0,3,2,1:T(8,128)} fusion(bf16[24,2,192,2,769]{4,3,2,1,0:T(2,128)(2,1)} %param.3, s32[384,64]{0,1:T(8,128)S(1)} %multiply_remainder_fusion.1, s32[]{:T(128)S(6)} %select_n.42, pred[384,64]{0,1:T(32,128)(4,1)S(1)} %get-tuple-element.11, pred[384,64]{0,1:T(32,128)(4,1)S(1)} %get-tuple-element.12), kind=kOutput, calls=%fused_computation.2 | convolution fusion | flops 1814372352 | bytes 47345668 | tf_op jit(solution)/shard_map/pckfr,kl->lpcfr/dot_general | solution.py:51
  32.0 0.0 copy-start
  32.0 0.0 reduce-scatter.2.cloned.1.call-update
  32.0 0.7 copy-done
  32.7 0.1 dynamic-slice_subtract_fusion
  32.7 0.2 iota_compare_fusion
  33.0 0.2 add_convert_fusion
  33.2 245.5 %reduce-scatter.2.cloned.1.call-done = f32[32,24,2,2,769]{4,0,3,2,1:T(8,128)} async-done(((f32[64,24,2,2,769]{4,0,3,2,1:T(8,128)}), f32[32,24,2,2,769]{4,0,3,2,1:T(8,128)}) %reduce-scatter.2.cloned.1.call-update) | async-done | bytes 9449488 | tf_op jit(solution)/shard_map/reduce_scatter | solution.py:50
  278.7 7.5 convert_bitcast_fusion
  286.1 51.0 %fusion.4 = bf16[24,2,2,32,2,1152]{5,3,4,2,1,0:T(8,128)(2,1)} fusion(bf16[24,769,1152,1,1,1]{2,0,1,5,4,3:T(8,128)(2,1)} %bitcast.18, bf16[24,2,769]{2,1,0:T(2,128)(2,1)S(1)} %add_convert_fusion, bf16[24,2,32,2,769]{4,2,3,1,0:T(8,128)(2,1)} %convert_bitcast_fusion), kind=kOutput, calls=%fused_computation.5 | convolution fusion | flops 10897594368 | bytes 61476960 | tf_op jit(solution)/shard_map/phclfr,prt->phclft/dot_general | solution.py:65
  337.1 20.9 %copy.38 = bf16[24,2,2,32,2,1152]{5,4,3,2,1,0:T(2,128)(2,1)} copy(bf16[24,2,2,32,2,1152]{5,3,4,2,1,0:T(8,128)(2,1)} %fusion.4) | data formatting | bytes 28311552 | tf_op jit(solution)/shard_map/convert_element_type | solution.py:67
  358.0 29.1 %reshape.152 = bf16[96,64,1152]{2,1,0:T(8,128)(2,1)} reshape(bf16[24,2,2,32,2,1152]{5,4,3,2,1,0:T(2,128)(2,1)} %copy.38) | data formatting | bytes 28311552 | tf_op jit(solution)/shard_map/reshape | solution.py:68
  387.1 25.5 %copy.39 = bf16[96,64,1152]{0,1,2:T(8,128)(2,1)} copy(bf16[96,64,1152]{2,1,0:T(8,128)(2,1)} %reshape.152) | data formatting | bytes 28311552 | tf_op jit(solution)/shard_map/reshape | solution.py:68
  412.6 6.5 all-to-all-start
  419.2 31.0 %multiply_convert_fusion.1 = (bf16[384,2,1,2304]{3,0,2,1:T(8,128)(2,1)S(1)}, bf16[384,2,1,2304]{3,0,2,1:T(8,128)(2,1)S(1)}) fusion(s32[384,2]{0,1:T(2,128)S(1)} %pad_add_fusion, f32[384,2]{0,1:T(2,128)S(1)} %get-tuple-element.7, f32[384,2]{0,1:T(2,128)S(1)} %get-tuple-element.8), kind=kLoop, calls=%fused_computation.12 | loop fusion | flops 23003136 | bytes 7087104 | tf_op jit(solution)/shard_map/convert
  450.2 0.6 pad_maximum_fusion
  450.9 21.2 %copy.42 = bf16[384,2,2,2304]{3,2,1,0:T(2,128)(2,1)} copy(bf16[384,2,2,2304]{3,0,2,1:T(8,128)(2,1)S(1)} %pad_maximum_fusion) | data formatting | bytes 14155776 | tf_op jit(solution)/shard_map/stack | solution.py:27
  472.1 15.2 %reshape.156 = bf16[1536,2304,1]{1,0,2:T(8,128)(2,1)} reshape(bf16[384,2,2,2304]{3,2,1,0:T(2,128)(2,1)} %copy.42) | data formatting | bytes 14155776 | tf_op jit(solution)/shard_map/convert_element_type | solution.py:28
  487.3 338.9 %all-to-all-done = bf16[96,64,1152]{0,1,2:T(8,128)(2,1)} async-done(((bf16[96,64,1152]{0,1,2:T(8,128)(2,1)}), bf16[96,64,1152]{0,1,2:T(8,128)(2,1)}, u32[]{:S(2)}, u32[]{:S(2)}) %all-to-all-start) | async-done | bytes 14155808 | tf_op jit(solution)/shard_map/all_to_all | solution.py:71
  826.2 20.6 %copy.41 = bf16[16,96,64,72]{1,0,3,2:T(8,128)(2,1)} copy(bf16[16,96,64,72]{1,2,3,0:T(8,128)(2,1)} %bitcast.6) | data formatting | bytes 28311552 | tf_op jit(solution)/shard_map/all_to_all | solution.py:71
  846.9 31.2 %all_to_all.16 = bf16[1536,64,72]{0,2,1:T(8,128)(2,1)} reshape(bf16[16,96,64,72]{1,0,3,2:T(8,128)(2,1)} %copy.41) | data formatting | bytes 28311552 | tf_op jit(solution)/shard_map/all_to_all | solution.py:71
  878.1 39.6 %convolution_convert_fusion = bf16[64,72,2304]{2,1,0:T(8,128)(2,1)} fusion(bf16[1536,64,72]{0,2,1:T(8,128)(2,1)} %all_to_all.16, bf16[1536,2304,1]{1,0,2:T(8,128)(2,1)} %reshape.156), kind=kOutput, calls=%fused_computation.4 | convolution fusion | flops 32625524736 | bytes 42467328 | tf_op jit(solution)/shard_map/oit,on->itn/dot_general | solution.py:69
  (6 shorter events, 0.1 us)
Async XLA Ops:
  6.5 272.1 %reduce-scatter.2.cloned.1.call-start = ((), (), s32[]{:S(2)}) async-start(), calls=%async_computation.2 | async-start | bytes 33030144 | tf_op jit(solution)/shard_map/reduce_scatter | solution.py:50
  32.0 0.7 copy-start
  412.6 413.6 %all-to-all-start = ((bf16[96,64,1152]{0,1,2:T(8,128)(2,1)}), bf16[96,64,1152]{0,1,2:T(8,128)(2,1)}, u32[]{:S(2)}, u32[]{:S(2)}) async-start(bf16[96,64,1152]{0,1,2:T(8,128)(2,1)} %copy.39), calls=%async_computation.1 | async-start | bytes 37748736 | tf_op jit(solution)/shard_map/all_to_all | solution.py:71
Sparse Core Ops, SparseCore 0:
  32.1 246.4 reduce-scatter.1
where the time goes:
time: 927 us; the launch traced here: 924 us
  waiting for transfers between devices  584 us (63%)
  local copies, waits for them, and re-layouts  164 us (18%)
  matrix products  116 us (13%)
  other arithmetic  39.8 us (4%)
  between operations  13.5 us (1%)
    all_to_all x1, waiting for transfers between devices, per_device(): lax.all_to_all(fourier, 'ma', split_axis=2, concat_axis=0, tiled=True)  339 us
    reduce_scatter x1, waiting for transfers between devices, per_device(): lax.psum_scatter(jnp.einsum('pckfr,kl->lpcfr', spectral, own_rows, prefer...  245 us
    reshape x2, local copies, waits for them, and re-layouts, per_device(): fourier.reshape(pair_dev * 4, block_levels * fields, fourier.shape[-1])  54.6 us
    all_to_all x2, local copies, waits for them, and re-layouts, per_device(): lax.all_to_all(fourier, 'ma', split_axis=2, concat_axis=0, tiled=True)  51.9 us
    dot_general x1, matrix products, per_device(): jnp.einsum('phclfr,prt->phclft', masked, latitude_basis, preferred_elemen...  51 us
    dot_general x1, matrix products, per_device(): jnp.einsum('oit,on->itn', lax.all_to_all(fourier, 'ma', split_axis=2, con...  39.6 us
    another operation x1, other arithmetic  31 us
    dot_general x1, matrix products, per_device(): jnp.einsum('pckfr,kl->lpcfr', spectral, own_rows, preferred_element_type=...  25.3 us
  transfers between devices with their start and end apart: 2, of which 2 were waited for; matrix products, arithmetic and copies ran while one was open for 7% of the time, Pallas kernels for 0%

commit v1 on v0

--- a/solution.py
+++ b/solution.py
@@ -3,7 +3,10 @@
 import jax
 import jax.numpy as jnp
 from jax import lax
+from jax.experimental import pallas as pl
+from jax.experimental.pallas import tpu as pltpu
 from jax.sharding import PartitionSpec as P
+
 
 NLON = 2304
 LEV = 64
@@ -15,6 +18,258 @@
     period = 2 * (total_modes - 1)
     phase_steps = mode_index * points % period
     return jnp.cos(phase_steps.astype(jnp.float32) * (2.0 * math.pi / period)).astype(jnp.bfloat16)
+
+
+def longitude_kernel(ca_ref, sa_ref, cb_ref, sb_ref, o_ref):
+    lanes = cb_ref.shape[1]
+    cb, sb = cb_ref[...], sb_ref[...]
+    for a in range(o_ref.shape[-1] // lanes):
+        ca, sa = ca_ref[:, a : a + 1], sa_ref[:, a : a + 1]
+        at = slice(a * lanes, (a + 1) * lanes)
+        o_ref[0, :, at] = (ca * cb - sa * sb).astype(jnp.bfloat16)
+        o_ref[1, :, at] = -(sa * cb + ca * sb).astype(jnp.bfloat16)
+
+
+def longitude_rows(pair_orders, degrees, points):
+    lanes = 128
+    orders = jnp.stack([pair_orders, degrees - 1 - pair_orders], axis=1).reshape(-1, 1)
+    weights = jnp.where(orders == 0, 1.0, 2.0).astype(jnp.float32)
+    column = lax.broadcasted_iota(jnp.int32, (1, lanes), 1)
+    unit = 2.0 * math.pi / points
+    coarse = ((orders * (column * lanes % points)) % points).astype(jnp.float32) * unit
+    fine = ((orders * column) % points).astype(jnp.float32) * unit
+    rows = orders.shape[0]
+    block = rows // 2
+    small = pl.BlockSpec((block, lanes), lambda i: (i, 0))
+    return pl.pallas_call(
+        longitude_kernel,
+        grid=(rows // block,),
+        in_specs=[small] * 4,
+        out_specs=pl.BlockSpec((2, block, points), lambda i: (0, i, 0)),
+        out_shape=jax.ShapeDtypeStruct((2, rows, points), jnp.bfloat16),
+        compiler_params=pltpu.CompilerParams(vmem_limit_bytes=48 * 2**20),
+        name="longitude",
+    )(weights * jnp.cos(coarse), weights * jnp.sin(coarse), jnp.cos(fine), jnp.sin(fine))
+
+
+def fourier_kernel(order_ref, basis_ref, kept_ref, got_ref, o_ref, w_ref, m_ref, t_ref, *, start):
+    pairs, degrees = kept_ref.shape[0], basis_ref.shape[0] - 1
+    half = m_ref.shape[1] // 2
+    first = pl.program_id(0) * pairs + start
+
+    @pl.when(pl.program_id(1) == 0)
+    def _():
+        column = lax.broadcasted_iota(jnp.int32, (half, degrees), 1)
+        for p in range(pairs):
+            own = kept_ref[p].reshape(half, degrees + 1) + got_ref[p].reshape(half, degrees + 1).astype(jnp.float32)
+            own = own.astype(jnp.bfloat16).astype(jnp.float32)
+            t_ref[p] = own[:, degrees:]
+            own = own[:, :degrees]
+            below = column < degrees - order_ref[first + p]
+            m_ref[p, :half] = jnp.where(below, own, 0.0).astype(jnp.bfloat16)
+            m_ref[p, half:] = jnp.where(below, 0.0, own).astype(jnp.bfloat16)
+
+    rows = 32
+
+    def turn(k, carry):
+        at = pl.multiple_of(k * rows, rows)
+        x = basis_ref[pl.ds(at, rows)].astype(jnp.float32)
+        w_ref[:, pl.ds(at, rows), :] = jnp.transpose(x, (1, 0, 2)).astype(jnp.bfloat16)
+        return carry
+
+    lax.fori_loop(0, degrees // rows, turn, 0)
+    last = basis_ref[degrees].astype(jnp.float32)
+    for p in range(pairs):
+        sums = jnp.dot(m_ref[p], w_ref[p], preferred_element_type=jnp.float32)
+        tail = t_ref[p] * last[p : p + 1]
+        o_ref[p, 0] = sums[:half].astype(jnp.bfloat16).reshape(o_ref.shape[2:])
+        o_ref[p, 1] = (sums[half:] + tail).astype(jnp.bfloat16).reshape(o_ref.shape[2:])
+
+
+def fourier_rows(kept, got, basis, orders, start, level_block):
+    pairs, parts, fields, levels, packed = got.shape
+    degrees, lat = packed - 1, basis.shape[2]
+    width, eight = lat // 3, 8
+    block = (eight, parts, fields, levels, packed)
+    return pl.pallas_call(
+        lambda *refs: fourier_kernel(*refs, start=start),
+        grid_spec=pltpu.PrefetchScalarGridSpec(
+            num_scalar_prefetch=1,
+            grid=(pairs // eight, lat // width),
+            in_specs=[
+                pl.BlockSpec((packed, eight, width), lambda g, t, _: (0, g + start // eight, t)),
+                pl.BlockSpec(block, lambda g, t, _: (g + start // eight, 0, 0, level_block, 0)),
+                pl.BlockSpec(block, lambda g, t, _: (g, 0, 0, 0, 0)),
+            ],
+            out_specs=pl.BlockSpec((eight, 2, parts, fields, levels, width), lambda g, t, _: (g, 0, 0, 0, 0, t)),
+            scratch_shapes=[
+                pltpu.VMEM((eight, degrees, width), jnp.bfloat16),
+                pltpu.VMEM((eight, 2 * parts * fields * levels, degrees), jnp.bfloat16),
+                pltpu.VMEM((eight, parts * fields * levels, 1), jnp.float32),
+            ],
+        ),
+        out_shape=jax.ShapeDtypeStruct((pairs, 2, parts, fields, levels, lat), jnp.bfloat16),
+        compiler_params=pltpu.CompilerParams(vmem_limit_bytes=56 * 2**20),
+        name="fourier",
+    )(orders, basis, kept, got)
+
+
+def pack_kernel(x_ref, *refs, dests, lats, fields):
+    outs, s_ref = refs[:-1], refs[-1]
+    rows, parts, series, _ = x_ref.shape
+    levels = series // fields
+
+    def turn(at, carry):
+        c, k = at // (rows // 8), pl.multiple_of(at % (rows // 8) * 8, 8)
+        block = jnp.transpose(x_ref[pl.ds(k, 8), c].astype(jnp.float32), (1, 0, 2))
+        for i in range(series):
+            s_ref[i, c, pl.ds(k, 8), :] = block[i % fields * levels + i // fields]
+        return carry
+
+    lax.fori_loop(0, parts * (rows // 8), turn, 0)
+    each = outs[0].shape[1]
+    group = series // (each * len(outs))
+    for n, o_ref in enumerate(outs):
+
+        def spread(at, carry):
+            g, c = at // parts, at % parts
+            for i in range(group):
+                whole = s_ref[(n * each + g) * group + i, c].astype(jnp.bfloat16)
+                for d in range(dests):
+                    o_ref[d, g, c, :, i * lats : (i + 1) * lats] = whole[:, d * lats : (d + 1) * lats]
+            return carry
+
+        lax.fori_loop(0, each * parts, spread, 0)
+
+
+def pack(fourier, dests, fields, groups, arrays):
+    rows, parts, series, lat = fourier.shape
+    lats = lat // dests
+    block = 16
+    shape = (dests, groups // arrays, parts, rows, series // groups * lats)
+    return pl.pallas_call(
+        lambda x, *refs: pack_kernel(x, *refs, dests=dests, lats=lats, fields=fields),
+        grid=(rows // block,),
+        in_specs=[pl.BlockSpec((block, parts, series, lat), lambda k: (k, 0, 0, 0))],
+        out_specs=[pl.BlockSpec(shape[:3] + (block, shape[4]), lambda k: (0, 0, 0, k, 0))] * arrays,
+        out_shape=[jax.ShapeDtypeStruct(shape, jnp.bfloat16)] * arrays,
+        scratch_shapes=[pltpu.VMEM((series, parts, block, lat), jnp.float32)],
+        compiler_params=pltpu.CompilerParams(vmem_limit_bytes=56 * 2**20),
+        name="pack",
+    )(fourier)
+
+
+def synth_kernel(*refs, parts):
+    table_ref, out_ref, lhs_ref = refs[parts], *refs[-2:]
+
+    @pl.when(pl.program_id(0) == 0)
+    def _():
+        at = 0
+        for c in range(2):
+            for ref in refs[:parts]:
+                rows = ref.shape[3]
+                few = 128 // rows
+                for s in range(0, ref.shape[0], few):
+                    x = ref[s : s + few, 0, c].reshape(128, -1)
+                    lhs_ref[:, at : at + 128] = jnp.transpose(x)
+                    at += 128
+
+    size = lhs_ref.shape[0] // 3
+
+    def some(m, carry):
+        at = pl.multiple_of(m * size, size)
+        out_ref[pl.ds(at, size), :] = jnp.dot(
+            lhs_ref[pl.ds(at, size), :], table_ref[...], preferred_element_type=jnp.float32
+        ).astype(jnp.bfloat16)
+        return carry
+
+    lax.fori_loop(0, 3, some, 0)
+
+
+def synthesize(data, table, out, group, groups):
+    lanes = data[0][0].shape[-1]
+    rows, points = table.shape
+    width = 256
+    in_specs, operands = [], []
+    for x, at in data:
+        in_specs.append(pl.BlockSpec((x.shape[0], 1) + x.shape[2:], lambda n, at=at: (0, at, 0, 0, 0)))
+        operands.append(x)
+    in_specs.append(pl.BlockSpec((rows, width), lambda n: (0, n)))
+    operands.append(table)
+    parts = len(data)
+    aliases = {}
+    if out is not None:
+        aliases = {len(operands): 0}
+        in_specs.append(pl.BlockSpec(memory_space=pl.ANY))
+        operands.append(out)
+    return pl.pallas_call(
+        lambda *refs: synth_kernel(*refs, parts=parts),
+        grid=(points // width,),
+        in_specs=in_specs,
+        out_specs=pl.BlockSpec((lanes, width), lambda n: (group, n)),
+        out_shape=jax.ShapeDtypeStruct((groups * lanes, points), jnp.bfloat16),
+        scratch_shapes=[pltpu.VMEM((lanes, rows), jnp.bfloat16)],
+        input_output_aliases=aliases,
+        compiler_params=pltpu.CompilerParams(vmem_limit_bytes=56 * 2**20),
+        name="synth",
+    )(*operands)
+
+
+def chunked(spectral, latitude_basis):
+    pairs, lats = spectral.shape[0], latitude_basis.shape[2] // lax.axis_size("ma")
+    return lax.axis_size("row") == 2 and lats % 8 == 0 and pairs % 8 == 0 and pairs > 8
+
+
+def per_device(spectral, latitude_basis, pair_orders):
+    if chunked(spectral, latitude_basis):
+        return per_device_chunked(spectral, latitude_basis, pair_orders)
+    return per_device_plain(spectral, latitude_basis, pair_orders)
+
+
+def per_device_chunked(spectral, latitude_basis, pair_orders):
+    pair_dev, _, local_modes, fields, packed = spectral.shape
+    degrees = packed - 1
+    lat = latitude_basis.shape[2]
+    row_count = lax.axis_size("row")
+    ma_count = lax.axis_size("ma")
+    level_dev = LEV // row_count
+    row = lax.axis_index("row")
+    mine = lax.axis_index("ma")
+    table = radial_table(local_modes * row_count, LEV)
+    own_rows = lax.dynamic_slice_in_dim(table, row * local_modes, local_modes, 0)
+    own_levels = lax.dynamic_slice_in_dim(own_rows, row * level_dev, level_dev, 1)
+    peer_levels = lax.dynamic_slice_in_dim(own_rows, (1 - row) * level_dev, level_dev, 1)
+    local_orders = lax.dynamic_slice_in_dim(pair_orders, mine * pair_dev, pair_dev, 0)
+    swap = [(0, 1), (1, 0)]
+
+    def radial(columns):
+        return jnp.einsum("pckfr,kl->pcflr", spectral, columns, preferred_element_type=jnp.float32)
+
+    sent = radial(peer_levels).astype(jnp.bfloat16)
+    kept = radial(own_levels)
+    basis = jnp.transpose(latitude_basis, (1, 0, 2))
+    groups = 4
+    half, eight = level_dev // 2, 8
+    chunks = [((0, eight), 0, 1), ((0, eight), 1, 1), ((eight, pair_dev), 0, 1), ((eight, pair_dev), 1, 2)]
+
+    def exchange(x):
+        return lax.all_to_all(x, "ma", split_axis=0, concat_axis=0, tiled=True)
+
+    got = []
+    for p, l, arrays in chunks:
+        peer = lax.ppermute(sent[p[0] : p[1], :, :, l * half : (l + 1) * half], "row", swap)
+        sums = fourier_rows(kept, peer, basis, local_orders, p[0], l)
+        sums = sums.reshape((p[1] - p[0]) * 2, 2, fields * half, lat)
+        packed_rows = pack(sums, ma_count, fields, groups // 2, arrays)
+        got += [exchange(x) for x in packed_rows]
+    by_owner = pair_orders.reshape(ma_count, pair_dev)
+    order_rows = jnp.concatenate([by_owner[:, :eight].reshape(-1), by_owner[:, eight:].reshape(-1)])
+    table = longitude_rows(order_rows, degrees, NLON).reshape(-1, NLON)
+    out = None
+    for g in range(groups):
+        data = [(got[g // 2], g % 2), (got[2], g) if g < 2 else (got[1 + g], 0)]
+        out = synthesize(data, table, out, g, groups)
+    return out.reshape(level_dev, fields, lat // ma_count, NLON)
 
 
 def longitude_table(pair_orders, degrees, points):
@@ -34,7 +289,7 @@
     return jnp.stack([below_split, jnp.logical_not(below_split)], axis=1).astype(jnp.bfloat16)
 
 
-def per_device(spectral, latitude_basis, pair_orders):
+def per_device_plain(spectral, latitude_basis, pair_orders):
     pair_dev = spectral.shape[0]
     local_modes = spectral.shape[2]
     fields = spectral.shape[3]

time: 927 us -> 497 us (0.54)
  waiting for transfers between devices: 584 us -> 110 us
  Pallas kernels: 0 us -> 193 us
  local copies, waits for them, and re-layouts: 164 us -> 11.1 us
  blocking collectives: 0 us -> 110 us
  matrix products: 116 us -> 39.6 us
  other arithmetic: 39.8 us -> 3.69 us
  starting transfers between devices: 6.54 us -> 27.9 us
  between operations: 13.5 us -> 0.11 us
    all_to_all x1 -> x4, waiting for transfers between devices: 339 us -> 8.36 us  [exchange(): return lax.all_to_all(x, 'ma', split_axis=0, concat_axis=0, tiled=True)]
    reduce_scatter x1 -> x0, waiting for transfers between devices: 245 us -> none  [per_device(): lax.psum_scatter(jnp.einsum('pckfr,kl->lpcfr', spectral, own_rows, prefer...]
    pallas_call x0 -> x13, Pallas kernels: none -> 193 us  [the longest x4 85.2 us: fourier_rows(): pl.pallas_call(lambda *refs: fourier_kernel(*refs, start=start), grid_spe...]
    all_to_all x0 -> x1, blocking collectives: none -> 110 us  [exchange(): return lax.all_to_all(x, 'ma', split_axis=0, concat_axis=0, tiled=True)]
    ppermute x0 -> x4, waiting for transfers between devices: none -> 101 us  [per_device_chunked(): lax.ppermute(sent[p[0]:p[1], :, :, l * half:(l + 1) * half], 'row', swap)]
    dot_general x3 -> x2, matrix products: 116 us -> 39.6 us  [radial(): jnp.einsum('pckfr,kl->pcflr', spectral, columns, preferred_element_type=j...]
    reshape x2 -> x4, local copies, waits for them, and re-layouts: 54.6 us -> 0.39 us  [the longest x1 0.15 us: longitude_rows(): jnp.stack([pair_orders, degrees - 1 - pair_orders], axis=1).reshape(-1, 1)]
    all_to_all x2 -> x0, local copies, waits for them, and re-layouts: 51.9 us -> none  [per_device(): lax.all_to_all(fourier, 'ma', split_axis=2, concat_axis=0, tiled=True)]
  transfers between devices with their start and end apart: 2 -> 8, of which waited for: 2 -> 4; matrix products, arithmetic and copies ran while one was open for 7% -> 6% of each run, Pallas kernels for 0% -> 31%
where the time goes in v1:
time: 497 us; the launch traced here: 495 us
  Pallas kernels  193 us (39%)
  waiting for transfers between devices  110 us (22%)
  blocking collectives  110 us (22%)
  matrix products  39.6 us (8%)
  starting transfers between devices  27.9 us (6%)
  local copies, waits for them, and re-layouts  11.1 us (2%)
    all_to_all x1, blocking collectives, exchange(): return lax.all_to_all(x, 'ma', split_axis=0, concat_axis=0, tiled=True)  110 us
    ppermute x4, waiting for transfers between devices, per_device_chunked(): lax.ppermute(sent[p[0]:p[1], :, :, l * half:(l + 1) * half], 'row', swap)  101 us
    pallas_call x4, Pallas kernels, fourier_rows(): pl.pallas_call(lambda *refs: fourier_kernel(*refs, start=start), grid_spe...  85.2 us
    pallas_call x4, Pallas kernels, synthesize(): pl.pallas_call(lambda *refs: synth_kernel(*refs, parts=parts), grid=(poin...  68.5 us
    dot_general x2, matrix products, radial(): jnp.einsum('pckfr,kl->pcflr', spectral, columns, preferred_element_type=j...  39.6 us
    pallas_call x4, Pallas kernels, pack(): pl.pallas_call(lambda x, *refs: pack_kernel(x, *refs, dests=dests, lats=l...  33.4 us
    all_to_all x4, starting transfers between devices, exchange(): return lax.all_to_all(x, 'ma', split_axis=0, concat_axis=0, tiled=True)  23.7 us
  transfers between devices with their start and end apart: 8, of which 4 were waited for; matrix products, arithmetic and copies ran while one was open for 6% of the time, Pallas kernels for 31%

profile of v1, /device:TPU:13, one launch (start us, length us, event | category | flops | bytes accessed | tf_op | source)
XLA Modules:
  0.0 495.3 jit_solution(2609105399342962528)
XLA Ops:
  0.4 19.4 %convert_bitcast_fusion = bf16[24,2,2,32,769]{4,3,2,1,0:T(8,128)(2,1)} fusion(bf16[24,2,192,2,769]{4,3,2,1,0:T(2,128)(2,1)} %param.3, bf16[384,64]{0,1:T(8,128)(2,1)S(1)} %fusion.24, s32[]{:T(128)S(6)} %select_n.60, s32[]{:T(128)S(6)} %select_n.64), kind=kOutput, calls=%fused_computation.4 | convolution fusion | flops 909511680 | bytes 33089544 | tf_op jit(solution)/shard_map/pckfr,kl->pcflr/dot_general | solution.py:246
  22.7 20.2 %fusion.4.refs_2_ = f32[24,2,2,32,769]{4,3,2,1,0:T(8,128)} fusion(bf16[24,2,192,2,769]{4,3,2,1,0:T(2,128)(2,1)} %param.3, bf16[384,64]{0,1:T(8,128)(2,1)S(1)} %fusion.24, s32[]{:T(128)S(6)} %select_n.60, s32[]{:T(128)S(6)} %select_n.62), kind=kOutput, calls=%fused_computation.5 | convolution fusion | flops 907149312 | bytes 37814280 | tf_op jit(solution)/shard_map/pckfr,kl->pcflr/dot_general | solution.py:246
  44.5 15.9 %fourier.6 = bf16[8,2,2,2,16,1152]{5,4,3,2,1,0:T(8,128)(2,1)} custom-call(s32[24]{0:T(128)} %dynamic_slice.10.refs_0_, bf16[769,24,1152]{2,1,0:T(8,128)(2,1)} %bitcast.22, f32[24,2,2,32,769]{4,3,2,1,0:T(8,128)} %fusion.4.refs_2_, bf16[8,2,2,16,769]{4,3,2,1,0:T(8,128)(2,1)} %copy-done.4), custom_call_target="tpu_custom_call" | custom-call | tf_op jit(solution)/shard_map/fourier/pallas_call | solution.py:94
  60.4 6.6 %pack.6 = bf16[16,2,2,16,1152]{4,3,2,1,0:T(8,128)(2,1)} custom-call(bf16[16,2,32,1152]{3,2,1,0:T(8,128)(2,1)} %bitcast.32), custom_call_target="tpu_custom_call" | custom-call | tf_op jit(solution)/shard_map/pack/pallas_call | solution.py:150
  67.0 6.8 %all-to-all-start.3 = ((bf16[16,2,2,16,1152]{4,3,2,1,0:T(8,128)(2,1)}), bf16[16,2,2,16,1152]{4,3,2,1,0:T(8,128)(2,1)S(1)}, u32[]{:S(2)}, u32[]{:S(2)}) async-start(bf16[16,2,2,16,1152]{4,3,2,1,0:T(8,128)(2,1)} %pack.6), calls=%async_computation.3 | async-start | bytes 4718592 | tf_op jit(solution)/shard_map/all_to_all | solution.py:256
  74.8 20.6 %collective-permute-done.refs_3_ = bf16[8,2,2,16,769]{4,3,2,1,0:T(8,128)(2,1)S(1)} collective-permute-done((bf16[8,2,2,16,769]{4,3,2,1,0:T(8,128)(2,1)S(1)}, bf16[8,2,2,16,769]{4,3,2,1,0:T(8,128)(2,1)S(1)}, u32[]{:S(2)}, u32[]{:S(2)}) %collective-permute-start) | collective-permute-done | bytes 787488 | tf_op jit(solution)/shard_map/ppermute | solution.py:260
  96.3 15.7 %fourier.4 = bf16[8,2,2,2,16,1152]{5,4,3,2,1,0:T(8,128)(2,1)} custom-call(s32[24]{0:T(128)} %dynamic_slice.10.refs_0_, bf16[769,24,1152]{2,1,0:T(8,128)(2,1)} %bitcast.23, f32[24,2,2,32,769]{4,3,2,1,0:T(8,128)} %fusion.4.refs_2_, bf16[8,2,2,16,769]{4,3,2,1,0:T(8,128)(2,1)} %copy-done.5), custom_call_target="tpu_custom_call" | custom-call | tf_op jit(solution)/shard_map/fourier/pallas_call | solution.py:94
  111.9 6.6 %pack.4 = bf16[16,2,2,16,1152]{4,3,2,1,0:T(8,128)(2,1)} custom-call(bf16[16,2,32,1152]{3,2,1,0:T(8,128)(2,1)} %bitcast.33), custom_call_target="tpu_custom_call" | custom-call | tf_op jit(solution)/shard_map/pack/pallas_call | solution.py:150
  118.5 8.3 %all-to-all-done.3.refs_0_ = bf16[16,2,2,16,1152]{4,3,2,1,0:T(8,128)(2,1)S(1)} async-done(((bf16[16,2,2,16,1152]{4,3,2,1,0:T(8,128)(2,1)}), bf16[16,2,2,16,1152]{4,3,2,1,0:T(8,128)(2,1)S(1)}, u32[]{:S(2)}, u32[]{:S(2)}) %all-to-all-start.3) | async-done | bytes 2359328 | tf_op jit(solution)/shard_map/all_to_all | solution.py:256
  126.9 4.8 all-to-all-start
  136.2 40.2 %collective-permute-done.1.refs_3_ = bf16[16,2,2,16,769]{4,3,2,1,0:T(8,128)(2,1)S(1)} collective-permute-done((bf16[16,2,2,16,769]{4,3,2,1,0:T(8,128)(2,1)S(1)}, bf16[16,2,2,16,769]{4,3,2,1,0:T(8,128)(2,1)S(1)}, u32[]{:S(2)}, u32[]{:S(2)}) %collective-permute-start.1) | collective-permute-done | bytes 1574944 | tf_op jit(solution)/shard_map/ppermute | solution.py:260
  177.7 26.9 %fourier.5 = bf16[16,2,2,2,16,1152]{5,4,3,2,1,0:T(8,128)(2,1)} custom-call(s32[24]{0:T(128)} %dynamic_slice.10.refs_0_, bf16[769,24,1152]{2,1,0:T(8,128)(2,1)} %bitcast.24, f32[24,2,2,32,769]{4,3,2,1,0:T(8,128)} %fusion.4.refs_2_, bf16[16,2,2,16,769]{4,3,2,1,0:T(8,128)(2,1)} %copy-done.3), custom_call_target="tpu_custom_call" | custom-call | tf_op jit(solution)/shard_map/fourier/pallas_call | solution.py:94
  204.6 10.1 %pack.5 = (bf16[16,1,2,32,1152]{4,3,2,1,0:T(8,128)(2,1)}, bf16[16,1,2,32,1152]{4,3,2,1,0:T(8,128)(2,1)}) custom-call(bf16[32,2,32,1152]{3,2,1,0:T(8,128)(2,1)} %bitcast.30), custom_call_target="tpu_custom_call" | custom-call | tf_op jit(solution)/shard_map/pack/pallas_call | solution.py:150
  214.7 6.9 %all-to-all-start.2 = ((bf16[16,1,2,32,1152]{4,3,2,1,0:T(8,128)(2,1)}), bf16[16,1,2,32,1152]{4,3,2,1,0:T(8,128)(2,1)S(1)}, u32[]{:S(2)}, u32[]{:S(2)}) async-start(bf16[16,1,2,32,1152]{4,3,2,1,0:T(8,128)(2,1)} %get-tuple-element.8), calls=%async_computation.2 | async-start | bytes 4718592 | tf_op jit(solution)/shard_map/all_to_all | solution.py:256
  222.5 40.4 %collective-permute-done.3.refs_3_ = bf16[16,2,2,16,769]{4,3,2,1,0:T(8,128)(2,1)S(1)} collective-permute-done((bf16[16,2,2,16,769]{4,3,2,1,0:T(8,128)(2,1)}, bf16[16,2,2,16,769]{4,3,2,1,0:T(8,128)(2,1)S(1)}, u32[]{:S(2)}, u32[]{:S(2)}) %collective-permute-start.3) | collective-permute-done | bytes 1574944 | tf_op jit(solution)/shard_map/ppermute | solution.py:260
  264.3 26.8 %fourier.7 = bf16[16,2,2,2,16,1152]{5,4,3,2,1,0:T(8,128)(2,1)} custom-call(s32[24]{0:T(128)} %dynamic_slice.10.refs_0_, bf16[769,24,1152]{2,1,0:T(8,128)(2,1)} %bitcast.25, f32[24,2,2,32,769]{4,3,2,1,0:T(8,128)} %fusion.4.refs_2_, bf16[16,2,2,16,769]{4,3,2,1,0:T(8,128)(2,1)} %copy-done.2), custom_call_target="tpu_custom_call" | custom-call | tf_op jit(solution)/shard_map/fourier/pallas_call | solution.py:94
  291.1 10.1 %pack.7 = bf16[16,2,2,32,1152]{4,3,2,1,0:T(8,128)(2,1)} custom-call(bf16[32,2,32,1152]{3,2,1,0:T(8,128)(2,1)} %bitcast.31), custom_call_target="tpu_custom_call" | custom-call | tf_op jit(solution)/shard_map/pack/pallas_call | solution.py:150
  301.2 110.4 %all_to_all.25.refs_1_ = bf16[16,2,2,32,1152]{4,3,2,1,0:T(8,128)(2,1)} all-to-all(bf16[16,2,2,32,1152]{4,3,2,1,0:T(8,128)(2,1)} %pack.7), channel_id=1, replica_groups=mesh['ma'=16,'row'=2] {'ma'}, dimensions={0} | all-to-all | bytes 9437184 | tf_op jit(solution)/shard_map/all_to_all | solution.py:256
  411.6 5.3 %all-to-all-start.1 = ((bf16[16,1,2,32,1152]{4,3,2,1,0:T(8,128)(2,1)}), bf16[16,1,2,32,1152]{4,3,2,1,0:T(8,128)(2,1)}, u32[]{:S(2)}, u32[]{:S(2)}) async-start(bf16[16,1,2,32,1152]{4,3,2,1,0:T(8,128)(2,1)} %get-tuple-element.7), calls=%async_computation.1 | async-start | bytes 4718592 | tf_op jit(solution)/shard_map/all_to_all | solution.py:256
  421.0 5.8 %longitude.1 = bf16[2,768,2304]{2,1,0:T(8,128)(2,1)} custom-call(f32[768,128]{1,0:T(8,128)S(1)} %get-tuple-element.14.ca_ref, f32[768,128]{1,0:T(8,128)S(1)} %get-tuple-element.13.sa_ref, f32[768,128]{1,0:T(8,128)S(1)} %get-tuple-element.16.cb_ref, f32[768,128]{1,0:T(8,128)S(1)} %get-tuple-element.15.sb_ref), custom_call_target="tpu_custom_call" | custom-call | tf_op jit(solution)/shard_map/longitude/pallas_call | solution.py:44
  426.8 17.1 %synth.4.refs_3_ = bf16[4608,2304]{1,0:T(8,128)(2,1)} custom-call(bf16[16,2,2,16,1152]{4,3,2,1,0:T(8,128)(2,1)} %copy-done, bf16[16,2,2,32,1152]{4,3,2,1,0:T(8,128)(2,1)} %all_to_all.25.refs_1_, bf16[1536,2304]{1,0:T(8,128)(2,1)} %bitcast.26), custom_call_target="tpu_custom_call" | custom-call | tf_op jit(solution)/shard_map/synth/pallas_call | solution.py:205
  444.0 17.1 %synth.5.refs_3_ = bf16[4608,2304]{1,0:T(8,128)(2,1)} custom-call(bf16[16,2,2,16,1152]{4,3,2,1,0:T(8,128)(2,1)} %copy-done, bf16[16,2,2,32,1152]{4,3,2,1,0:T(8,128)(2,1)} %all_to_all.25.refs_1_, bf16[1536,2304]{1,0:T(8,128)(2,1)} %bitcast.27, bf16[4608,2304]{1,0:T(8,128)(2,1)} %synth.4.refs_3_), custom_call_target="tpu_custom_call", output_to_operand_aliasing={{}: (3, {})} | custom-call | tf_op jit(solution)/shard_map/synth/pallas_call | solution.py:205
  461.1 17.1 %synth.6.refs_3_ = bf16[4608,2304]{1,0:T(8,128)(2,1)} custom-call(bf16[16,2,2,16,1152]{4,3,2,1,0:T(8,128)(2,1)} %all-to-all-done.refs_0_, bf16[16,1,2,32,1152]{4,3,2,1,0:T(8,128)(2,1)} %copy-done.1, bf16[1536,2304]{1,0:T(8,128)(2,1)} %bitcast.28, bf16[4608,2304]{1,0:T(8,128)(2,1)} %synth.5.refs_3_), custom_call_target="tpu_custom_call", output_to_operand_aliasing={{}: (3, {})} | custom-call | tf_op jit(solution)/shard_map/synth/pallas_call | solution.py:205
  478.2 17.1 %synth.7 = bf16[4608,2304]{1,0:T(8,128)(2,1)} custom-call(bf16[16,2,2,16,1152]{4,3,2,1,0:T(8,128)(2,1)} %all-to-all-done.refs_0_, bf16[16,1,2,32,1152]{4,3,2,1,0:T(8,128)(2,1)} %all-to-all-done.1.refs_1_, bf16[1536,2304]{1,0:T(8,128)(2,1)} %bitcast.29, bf16[4608,2304]{1,0:T(8,128)(2,1)} %synth.6.refs_3_), custom_call_target="tpu_custom_call", output_to_operand_aliasing={{}: (3, {})} | custom-call | tf_op jit(solution)/shard_map/synth/pallas_call | solution.py:205
  (41 shorter events, 19.0 us)
Async XLA Ops:
  21.4 22.1 %collective-permute-start.2 = (bf16[8,2,2,16,769]{4,3,2,1,0:T(8,128)(2,1)S(1)}, bf16[8,2,2,16,769]{4,3,2,1,0:T(8,128)(2,1)S(1)}, u32[]{:S(2)}, u32[]{:S(2)}) collective-permute-start(bf16[8,2,2,16,769]{4,3,2,1,0:T(8,128)(2,1)S(1)} %get-tuple-element.11), channel_id=1, source_target_pairs={{0,1},{1,0},{2,3},{3,2},{4,5},{5,4},{6,7},{7,6},{8,9},{9,8},{10,11... | collective-permute-start | bytes 2362376 | tf_op jit(solution)/shard_map/ppermute | solution.py:260
  22.7 20.2 %copy-start.6 = (s32[384]{0:T(512)S(1)}, s32[384]{0:T(512)}, u32[]{:S(2)}) copy-start(s32[384]{0:T(512)} %param.5) | copy-start | bytes 4612
  43.5 1.0 copy-start.4
  67.0 59.8 %all-to-all-start.3 = ((bf16[16,2,2,16,1152]{4,3,2,1,0:T(8,128)(2,1)}), bf16[16,2,2,16,1152]{4,3,2,1,0:T(8,128)(2,1)S(1)}, u32[]{:S(2)}, u32[]{:S(2)}) async-start(bf16[16,2,2,16,1152]{4,3,2,1,0:T(8,128)(2,1)} %pack.6), calls=%async_computation.3 | async-start | bytes 4718592 | tf_op jit(solution)/shard_map/all_to_all | solution.py:256
  73.8 21.5 %collective-permute-start = (bf16[8,2,2,16,769]{4,3,2,1,0:T(8,128)(2,1)S(1)}, bf16[8,2,2,16,769]{4,3,2,1,0:T(8,128)(2,1)S(1)}, u32[]{:S(2)}, u32[]{:S(2)}) collective-permute-start(bf16[8,2,2,16,769]{4,3,2,1,0:T(8,128)(2,1)S(1)} %get-tuple-element.12), channel_id=1, source_target_pairs={{0,1},{1,0},{2,3},{3,2},{4,5},{5,4},{6,7},{7,6},{8,9},{9,8},{10,11... | collective-permute-start | bytes 2362376 | tf_op jit(solution)/shard_map/ppermute | solution.py:260
  95.3 0.9 copy-start.5
  126.9 8.4 %copy-start = (bf16[16,2,2,16,1152]{4,3,2,1,0:T(8,128)(2,1)}, bf16[16,2,2,16,1152]{4,3,2,1,0:T(8,128)(2,1)S(1)}, u32[]{:S(2)}) copy-start(bf16[16,2,2,16,1152]{4,3,2,1,0:T(8,128)(2,1)S(1)} %all-to-all-done.3.refs_0_) | copy-start | bytes 7077892
  126.9 87.8 %all-to-all-start = ((bf16[16,2,2,16,1152]{4,3,2,1,0:T(8,128)(2,1)}), bf16[16,2,2,16,1152]{4,3,2,1,0:T(8,128)(2,1)}, u32[]{:S(2)}, u32[]{:S(2)}) async-start(bf16[16,2,2,16,1152]{4,3,2,1,0:T(8,128)(2,1)} %pack.4), calls=%async_computation | async-start | bytes 4718592 | tf_op jit(solution)/shard_map/all_to_all | solution.py:256
  135.2 41.2 %collective-permute-start.1 = (bf16[16,2,2,16,769]{4,3,2,1,0:T(8,128)(2,1)S(1)}, bf16[16,2,2,16,769]{4,3,2,1,0:T(8,128)(2,1)S(1)}, u32[]{:S(2)}, u32[]{:S(2)}) collective-permute-start(bf16[16,2,2,16,769]{4,3,2,1,0:T(8,128)(2,1)S(1)} %get-tuple-element.10), channel_id=1, source_target_pairs={{0,1},{1,0},{2,3},{3,2},{4,5},{5,4},{6,7},{7,6},{8,9},{9,8},{10,11... | collective-permute-start | bytes 4724744 | tf_op jit(solution)/shard_map/ppermute | solution.py:260
  176.4 1.3 copy-start.3
  214.7 86.5 %all-to-all-start.2 = ((bf16[16,1,2,32,1152]{4,3,2,1,0:T(8,128)(2,1)}), bf16[16,1,2,32,1152]{4,3,2,1,0:T(8,128)(2,1)S(1)}, u32[]{:S(2)}, u32[]{:S(2)}) async-start(bf16[16,1,2,32,1152]{4,3,2,1,0:T(8,128)(2,1)} %get-tuple-element.8), calls=%async_computation.2 | async-start | bytes 4718592 | tf_op jit(solution)/shard_map/all_to_all | solution.py:256
  221.6 41.4 %collective-permute-start.3 = (bf16[16,2,2,16,769]{4,3,2,1,0:T(8,128)(2,1)}, bf16[16,2,2,16,769]{4,3,2,1,0:T(8,128)(2,1)S(1)}, u32[]{:S(2)}, u32[]{:S(2)}) collective-permute-start(bf16[16,2,2,16,769]{4,3,2,1,0:T(8,128)(2,1)} %get-tuple-element.9), channel_id=1, source_target_pairs={{0,1},{1,0},{2,3},{3,2},{4,5},{5,4},{6,7},{7,6},{8,9},{9,8},{10,11... | collective-permute-start | bytes 4724744 | tf_op jit(solution)/shard_map/ppermute | solution.py:260
  263.0 1.3 copy-start.2
  301.2 110.4 %copy-start.1 = (bf16[16,1,2,32,1152]{4,3,2,1,0:T(8,128)(2,1)}, bf16[16,1,2,32,1152]{4,3,2,1,0:T(8,128)(2,1)S(1)}, u32[]{:S(2)}) copy-start(bf16[16,1,2,32,1152]{4,3,2,1,0:T(8,128)(2,1)S(1)} %all-to-all-done.2.refs_1_) | copy-start | bytes 7077892
  411.6 66.6 %all-to-all-start.1 = ((bf16[16,1,2,32,1152]{4,3,2,1,0:T(8,128)(2,1)}), bf16[16,1,2,32,1152]{4,3,2,1,0:T(8,128)(2,1)}, u32[]{:S(2)}, u32[]{:S(2)}) async-start(bf16[16,1,2,32,1152]{4,3,2,1,0:T(8,128)(2,1)} %get-tuple-element.7), calls=%async_computation.1 | async-start | bytes 4718592 | tf_op jit(solution)/shard_map/all_to_all | solution.py:256

commit v2 on v1

--- a/solution.py
+++ b/solution.py
@@ -162,7 +162,7 @@
 def synth_kernel(*refs, parts):
     table_ref, out_ref, lhs_ref = refs[parts], *refs[-2:]
 
-    @pl.when(pl.program_id(0) == 0)
+    @pl.when(pl.program_id(1) == 0)
     def _():
         at = 0
         for c in range(2):
@@ -186,15 +186,15 @@
     lax.fori_loop(0, 3, some, 0)
 
 
-def synthesize(data, table, out, group, groups):
+def synthesize(data, table, out, group, count, groups):
     lanes = data[0][0].shape[-1]
     rows, points = table.shape
     width = 256
     in_specs, operands = [], []
     for x, at in data:
-        in_specs.append(pl.BlockSpec((x.shape[0], 1) + x.shape[2:], lambda n, at=at: (0, at, 0, 0, 0)))
+        in_specs.append(pl.BlockSpec((x.shape[0], 1) + x.shape[2:], lambda g, n, at=at: (0, at + g, 0, 0, 0)))
         operands.append(x)
-    in_specs.append(pl.BlockSpec((rows, width), lambda n: (0, n)))
+    in_specs.append(pl.BlockSpec((rows, width), lambda g, n: (0, n)))
     operands.append(table)
     parts = len(data)
     aliases = {}
@@ -204,9 +204,9 @@
         operands.append(out)
     return pl.pallas_call(
         lambda *refs: synth_kernel(*refs, parts=parts),
-        grid=(points // width,),
+        grid=(count, points // width),
         in_specs=in_specs,
-        out_specs=pl.BlockSpec((lanes, width), lambda n: (group, n)),
+        out_specs=pl.BlockSpec((lanes, width), lambda g, n: (group + g, n)),
         out_shape=jax.ShapeDtypeStruct((groups * lanes, points), jnp.bfloat16),
         scratch_shapes=[pltpu.VMEM((lanes, rows), jnp.bfloat16)],
         input_output_aliases=aliases,
@@ -242,11 +242,13 @@
     local_orders = lax.dynamic_slice_in_dim(pair_orders, mine * pair_dev, pair_dev, 0)
     swap = [(0, 1), (1, 0)]
 
-    def radial(columns):
-        return jnp.einsum("pckfr,kl->pcflr", spectral, columns, preferred_element_type=jnp.float32)
-
-    sent = radial(peer_levels).astype(jnp.bfloat16)
-    kept = radial(own_levels)
+    def radial(coeffs, columns):
+        return jnp.einsum("pckfr,kl->pcflr", coeffs, columns, preferred_element_type=jnp.float32)
+
+    early = lax.optimization_barrier(spectral[:8])
+    sent0 = radial(early, peer_levels).astype(jnp.bfloat16)
+    kept0 = radial(early, own_levels)
+    both = radial(spectral, jnp.concatenate([peer_levels, own_levels], axis=1))
     basis = jnp.transpose(latitude_basis, (1, 0, 2))
     groups = 4
     half, eight = level_dev // 2, 8
@@ -257,8 +259,10 @@
 
     got = []
     for p, l, arrays in chunks:
-        peer = lax.ppermute(sent[p[0] : p[1], :, :, l * half : (l + 1) * half], "row", swap)
-        sums = fourier_rows(kept, peer, basis, local_orders, p[0], l)
+        sent, kept, kept_at = (both, both, l + 2) if p[0] else (sent0, kept0, l)
+        sent = sent[p[0] : p[1], :, :, l * half : (l + 1) * half].astype(jnp.bfloat16)
+        peer = lax.ppermute(sent, "row", swap)
+        sums = fourier_rows(kept, peer, basis, local_orders, p[0], kept_at)
         sums = sums.reshape((p[1] - p[0]) * 2, 2, fields * half, lat)
         packed_rows = pack(sums, ma_count, fields, groups // 2, arrays)
         got += [exchange(x) for x in packed_rows]
@@ -266,9 +270,9 @@
     order_rows = jnp.concatenate([by_owner[:, :eight].reshape(-1), by_owner[:, eight:].reshape(-1)])
     table = longitude_rows(order_rows, degrees, NLON).reshape(-1, NLON)
     out = None
-    for g in range(groups):
-        data = [(got[g // 2], g % 2), (got[2], g) if g < 2 else (got[1 + g], 0)]
-        out = synthesize(data, table, out, g, groups)
+    for at, (g, count) in enumerate(((0, 2), (2, 1), (3, 1))):
+        data = [(got[g // 2], g % 2), (got[2 + at], 0)]
+        out = synthesize(data, table, out, g, count, groups)
     return out.reshape(level_dev, fields, lat // ma_count, NLON)
 
 

time: 497 us -> 518 us (1.042)
  local copies, waits for them, and re-layouts: 11.1 us -> 23.2 us
  waiting for transfers between devices: 110 us -> 120 us
    ppermute x4, waiting for transfers between devices: 101 us -> 112 us  [per_device_chunked(): peer = lax.ppermute(sent, 'row', swap)]
    slice x2 -> x3, local copies, waits for them, and re-layouts: 5.21 us -> 13.8 us  [the longest x1 9.93 us: per_device_chunked(): early = lax.optimization_barrier(spectral[:8])]
    pallas_call x4 -> x3, Pallas kernels: 68.5 us -> 66.7 us  [synthesize(): pl.pallas_call(lambda *refs: synth_kernel(*refs, parts=parts), grid=(coun...]
    dot_general x2 -> x3, matrix products: 39.6 us -> 39.2 us  [radial(): jnp.einsum('pckfr,kl->pcflr', coeffs, columns, preferred_element_type=jnp...]
  transfers between devices with their start and end apart: 8 -> 8, of which waited for: 4 -> 5; matrix products, arithmetic and copies ran while one was open for 6% -> 9% of each run, Pallas kernels for 31% -> 29%
where the time goes in v2:
time: 518 us; the launch traced here: 517 us
  Pallas kernels  191 us (37%)
  waiting for transfers between devices  120 us (23%)
  blocking collectives  110 us (21%)
  matrix products  39.2 us (8%)
  starting transfers between devices  29.2 us (6%)
  local copies, waits for them, and re-layouts  23.2 us (4%)
    ppermute x4, waiting for transfers between devices, per_device_chunked(): peer = lax.ppermute(sent, 'row', swap)  112 us
    all_to_all x1, blocking collectives, exchange(): return lax.all_to_all(x, 'ma', split_axis=0, concat_axis=0, tiled=True)  110 us
    pallas_call x4, Pallas kernels, fourier_rows(): pl.pallas_call(lambda *refs: fourier_kernel(*refs, start=start), grid_spe...  84.8 us
    pallas_call x3, Pallas kernels, synthesize(): pl.pallas_call(lambda *refs: synth_kernel(*refs, parts=parts), grid=(coun...  66.7 us
    dot_general x3, matrix products, radial(): jnp.einsum('pckfr,kl->pcflr', coeffs, columns, preferred_element_type=jnp...  39.2 us
    pallas_call x4, Pallas kernels, pack(): pl.pallas_call(lambda x, *refs: pack_kernel(x, *refs, dests=dests, lats=l...  33.4 us
    all_to_all x4, starting transfers between devices, exchange(): return lax.all_to_all(x, 'ma', split_axis=0, concat_axis=0, tiled=True)  24.3 us
  transfers between devices with their start and end apart: 8, of which 5 were waited for; matrix products, arithmetic and copies ran while one was open for 9% of the time, Pallas kernels for 29%

profile of v2, /device:TPU:13, one launch (start us, length us, event | category | flops | bytes accessed | tf_op | source)
XLA Modules:
  0.0 516.7 jit_solution(7077035121589169720)
XLA Ops:
  0.4 9.9 %slice.23 = bf16[8,2,192,2,769]{4,3,2,1,0:T(2,128)(2,1)S(1)} slice(bf16[24,2,192,2,769]{4,3,2,1,0:T(2,128)(2,1)} %param.3), slice={[0:8], [0:2], [0:192], [0:2], [0:769]} | slice | bytes 18898944 | tf_op jit(solution)/shard_map/slice | solution.py:248
  16.8 8.1 %fusion.9.refs_2_ = f32[8,2,2,32,769]{4,3,2,1,0:T(8,128)} fusion(bf16[8,2,192,2,769]{4,3,2,1,0:T(2,128)(2,1)} %copy-done, bf16[192,32]{0,1:T(8,128)(2,1)S(1)} %get-tuple-element.14), kind=kOutput, calls=%fused_computation.7 | convolution fusion | flops 302383104 | bytes 12611584 | tf_op jit(solution)/shard_map/pckfr,kl->pcflr/dot_general | solution.py:246
  24.9 11.3 %collective-permute-done.refs_3_ = bf16[8,2,2,16,769]{4,3,2,1,0:T(8,128)(2,1)S(1)} collective-permute-done((bf16[8,2,2,16,769]{4,3,2,1,0:T(8,128)(2,1)S(1)}, bf16[8,2,2,16,769]{4,3,2,1,0:T(8,128)(2,1)S(1)}, u32[]{:S(2)}, u32[]{:S(2)}) %collective-permute-start) | collective-permute-done | bytes 787488 | tf_op jit(solution)/shard_map/ppermute | solution.py:264
  37.1 15.6 %fourier.4 = bf16[8,2,2,2,16,1152]{5,4,3,2,1,0:T(8,128)(2,1)} custom-call(s32[24]{0:T(128)} %dynamic_slice.10.refs_0_, bf16[769,24,1152]{2,1,0:T(8,128)(2,1)} %bitcast.31, f32[8,2,2,32,769]{4,3,2,1,0:T(8,128)} %fusion.9.refs_2_, bf16[8,2,2,16,769]{4,3,2,1,0:T(8,128)(2,1)} %copy-done.6), custom_call_target="tpu_custom_call" | custom-call | tf_op jit(solution)/shard_map/fourier/pallas_call | solution.py:94
  52.7 6.6 %pack.4 = bf16[16,2,2,16,1152]{4,3,2,1,0:T(8,128)(2,1)} custom-call(bf16[16,2,32,1152]{3,2,1,0:T(8,128)(2,1)} %bitcast.41), custom_call_target="tpu_custom_call" | custom-call | tf_op jit(solution)/shard_map/pack/pallas_call | solution.py:150
  59.3 7.4 %all-to-all-start = ((bf16[16,2,2,16,1152]{4,3,2,1,0:T(8,128)(2,1)}), bf16[16,2,2,16,1152]{4,3,2,1,0:T(8,128)(2,1)S(1)}, u32[]{:S(2)}, u32[]{:S(2)}) async-start(bf16[16,2,2,16,1152]{4,3,2,1,0:T(8,128)(2,1)} %pack.4), calls=%async_computation | async-start | bytes 4718592 | tf_op jit(solution)/shard_map/all_to_all | solution.py:258
  67.9 20.3 %collective-permute-done.2.refs_3_ = bf16[8,2,2,16,769]{4,3,2,1,0:T(8,128)(2,1)S(1)} collective-permute-done((bf16[8,2,2,16,769]{4,3,2,1,0:T(8,128)(2,1)S(1)}, bf16[8,2,2,16,769]{4,3,2,1,0:T(8,128)(2,1)S(1)}, u32[]{:S(2)}, u32[]{:S(2)}) %collective-permute-start.2) | collective-permute-done | bytes 787488 | tf_op jit(solution)/shard_map/ppermute | solution.py:264
  89.1 15.6 %fourier.6 = bf16[8,2,2,2,16,1152]{5,4,3,2,1,0:T(8,128)(2,1)} custom-call(s32[24]{0:T(128)} %dynamic_slice.10.refs_0_, bf16[769,24,1152]{2,1,0:T(8,128)(2,1)} %bitcast.32, f32[8,2,2,32,769]{4,3,2,1,0:T(8,128)} %fusion.9.refs_2_, bf16[8,2,2,16,769]{4,3,2,1,0:T(8,128)(2,1)} %copy-done.7), custom_call_target="tpu_custom_call" | custom-call | tf_op jit(solution)/shard_map/fourier/pallas_call | solution.py:94
  104.8 6.6 %pack.6 = bf16[16,2,2,16,1152]{4,3,2,1,0:T(8,128)(2,1)} custom-call(bf16[16,2,32,1152]{3,2,1,0:T(8,128)(2,1)} %bitcast.40), custom_call_target="tpu_custom_call" | custom-call | tf_op jit(solution)/shard_map/pack/pallas_call | solution.py:150
  111.3 8.4 %all-to-all-done.refs_0_ = bf16[16,2,2,16,1152]{4,3,2,1,0:T(8,128)(2,1)S(1)} async-done(((bf16[16,2,2,16,1152]{4,3,2,1,0:T(8,128)(2,1)}), bf16[16,2,2,16,1152]{4,3,2,1,0:T(8,128)(2,1)S(1)}, u32[]{:S(2)}, u32[]{:S(2)}) %all-to-all-start) | async-done | bytes 2359328 | tf_op jit(solution)/shard_map/all_to_all | solution.py:258
  124.5 28.9 %fusion.41 = (bf16[24,2,2,64,769]{4,3,2,1,0:T(8,128)(2,1)}, f32[24,2,2,64,769]{4,3,2,1,0:T(8,128)}) fusion(bf16[24,2,192,2,769]{4,3,2,1,0:T(2,128)(2,1)} %param.3, bf16[192,32]{0,1:T(8,128)(2,1)S(1)} %get-tuple-element.14, bf16[192,32]{0,1:T(8,128)(2,1)S(1)} %get-tuple-element.13), kind=kOutput, calls=%fused_computation.50 | convolution fusion | flops 1819072512 | bytes 56721408 | tf_op jit(solution)/shard_map/pckfr,kl->pcflr/dot_general | solution.py:246
  158.2 40.0 %collective-permute-done.1.refs_3_ = bf16[16,2,2,16,769]{4,3,2,1,0:T(8,128)(2,1)S(1)} collective-permute-done((bf16[16,2,2,16,769]{4,3,2,1,0:T(8,128)(2,1)S(1)}, bf16[16,2,2,16,769]{4,3,2,1,0:T(8,128)(2,1)S(1)}, u32[]{:S(2)}, u32[]{:S(2)}) %collective-permute-start.1) | collective-permute-done | bytes 1574944 | tf_op jit(solution)/shard_map/ppermute | solution.py:264
  199.4 26.7 %fourier.5 = bf16[16,2,2,2,16,1152]{5,4,3,2,1,0:T(8,128)(2,1)} custom-call(s32[24]{0:T(128)} %dynamic_slice.10.refs_0_, bf16[769,24,1152]{2,1,0:T(8,128)(2,1)} %bitcast.33, f32[24,2,2,64,769]{4,3,2,1,0:T(8,128)} %get-tuple-element.20.refs_2_, bf16[16,2,2,16,769]{4,3,2,1,0:T(8,128)(2,1)} %copy-done.5), custom_call_target="tpu_custom_call" | custom-call | tf_op jit(solution)/shard_map/fourier/pallas_call | solution.py:94
  226.2 10.2 %pack.5 = (bf16[16,1,2,32,1152]{4,3,2,1,0:T(8,128)(2,1)}, bf16[16,1,2,32,1152]{4,3,2,1,0:T(8,128)(2,1)}) custom-call(bf16[32,2,32,1152]{3,2,1,0:T(8,128)(2,1)} %bitcast.38), custom_call_target="tpu_custom_call" | custom-call | tf_op jit(solution)/shard_map/pack/pallas_call | solution.py:150
  236.4 6.9 %all-to-all-start.2 = ((bf16[16,1,2,32,1152]{4,3,2,1,0:T(8,128)(2,1)}), bf16[16,1,2,32,1152]{4,3,2,1,0:T(8,128)(2,1)S(1)}, u32[]{:S(2)}, u32[]{:S(2)}) async-start(bf16[16,1,2,32,1152]{4,3,2,1,0:T(8,128)(2,1)} %get-tuple-element.8), calls=%async_computation.2 | async-start | bytes 4718592 | tf_op jit(solution)/shard_map/all_to_all | solution.py:258
  244.5 40.2 %collective-permute-done.3.refs_3_ = bf16[16,2,2,16,769]{4,3,2,1,0:T(8,128)(2,1)S(1)} collective-permute-done((bf16[16,2,2,16,769]{4,3,2,1,0:T(8,128)(2,1)}, bf16[16,2,2,16,769]{4,3,2,1,0:T(8,128)(2,1)S(1)}, u32[]{:S(2)}, u32[]{:S(2)}) %collective-permute-start.3) | collective-permute-done | bytes 1574944 | tf_op jit(solution)/shard_map/ppermute | solution.py:264
  285.9 26.8 %fourier.7 = bf16[16,2,2,2,16,1152]{5,4,3,2,1,0:T(8,128)(2,1)} custom-call(s32[24]{0:T(128)} %dynamic_slice.10.refs_0_, bf16[769,24,1152]{2,1,0:T(8,128)(2,1)} %bitcast.34, f32[24,2,2,64,769]{4,3,2,1,0:T(8,128)} %get-tuple-element.20.refs_2_, bf16[16,2,2,16,769]{4,3,2,1,0:T(8,128)(2,1)} %copy-done.4), custom_call_target="tpu_custom_call" | custom-call | tf_op jit(solution)/shard_map/fourier/pallas_call | solution.py:94
  312.7 10.1 %pack.7 = bf16[16,2,2,32,1152]{4,3,2,1,0:T(8,128)(2,1)} custom-call(bf16[32,2,32,1152]{3,2,1,0:T(8,128)(2,1)} %bitcast.39), custom_call_target="tpu_custom_call" | custom-call | tf_op jit(solution)/shard_map/pack/pallas_call | solution.py:150
  322.8 110.4 %all_to_all.25.refs_1_ = bf16[16,2,2,32,1152]{4,3,2,1,0:T(8,128)(2,1)} all-to-all(bf16[16,2,2,32,1152]{4,3,2,1,0:T(8,128)(2,1)} %pack.7), channel_id=1, replica_groups=mesh['ma'=16,'row'=2] {'ma'}, dimensions={0} | all-to-all | bytes 9437184 | tf_op jit(solution)/shard_map/all_to_all | solution.py:258
  433.2 5.3 %all-to-all-start.1 = ((bf16[16,1,2,32,1152]{4,3,2,1,0:T(8,128)(2,1)}), bf16[16,1,2,32,1152]{4,3,2,1,0:T(8,128)(2,1)S(1)}, u32[]{:S(2)}, u32[]{:S(2)}) async-start(bf16[16,1,2,32,1152]{4,3,2,1,0:T(8,128)(2,1)} %get-tuple-element.7), calls=%async_computation.1 | async-start | bytes 4718592 | tf_op jit(solution)/shard_map/all_to_all | solution.py:258
  442.6 5.8 %longitude.1 = bf16[2,768,2304]{2,1,0:T(8,128)(2,1)} custom-call(f32[768,128]{1,0:T(8,128)S(1)} %get-tuple-element.16.ca_ref, f32[768,128]{1,0:T(8,128)S(1)} %get-tuple-element.15.sa_ref, f32[768,128]{1,0:T(8,128)S(1)} %get-tuple-element.18.cb_ref, f32[768,128]{1,0:T(8,128)S(1)} %get-tuple-element.17.sb_ref), custom_call_target="tpu_custom_call" | custom-call | tf_op jit(solution)/shard_map/longitude/pallas_call | solution.py:44
  448.4 32.5 %synth.3.refs_3_ = bf16[4608,2304]{1,0:T(8,128)(2,1)} custom-call(bf16[16,2,2,16,1152]{4,3,2,1,0:T(8,128)(2,1)} %all-to-all-done.3.refs_0_, bf16[16,2,2,32,1152]{4,3,2,1,0:T(8,128)(2,1)} %all_to_all.25.refs_1_, bf16[1536,2304]{1,0:T(8,128)(2,1)} %bitcast.35), custom_call_target="tpu_custom_call" | custom-call | tf_op jit(solution)/shard_map/synth/pallas_call | solution.py:205
  480.9 17.1 %synth.4.refs_3_ = bf16[4608,2304]{1,0:T(8,128)(2,1)} custom-call(bf16[16,2,2,16,1152]{4,3,2,1,0:T(8,128)(2,1)} %copy-done.1, bf16[16,1,2,32,1152]{4,3,2,1,0:T(8,128)(2,1)} %copy-done.2, bf16[1536,2304]{1,0:T(8,128)(2,1)} %bitcast.36, bf16[4608,2304]{1,0:T(8,128)(2,1)} %synth.3.refs_3_), custom_call_target="tpu_custom_call", output_to_operand_aliasing={{}: (3, {})} | custom-call | tf_op jit(solution)/shard_map/synth/pallas_call | solution.py:205
  499.6 17.1 %synth.5 = bf16[4608,2304]{1,0:T(8,128)(2,1)} custom-call(bf16[16,2,2,16,1152]{4,3,2,1,0:T(8,128)(2,1)} %copy-done.1, bf16[16,1,2,32,1152]{4,3,2,1,0:T(8,128)(2,1)} %copy-done.3, bf16[1536,2304]{1,0:T(8,128)(2,1)} %bitcast.37, bf16[4608,2304]{1,0:T(8,128)(2,1)} %synth.4.refs_3_), custom_call_target="tpu_custom_call", output_to_operand_aliasing={{}: (3, {})} | custom-call | tf_op jit(solution)/shard_map/synth/pallas_call | solution.py:205
  (47 shorter events, 28.7 us)
Async XLA Ops:
  10.4 4.3 copy-start
  10.5 5.7 %copy-start.8 = (s32[384]{0:T(512)S(1)}, s32[384]{0:T(512)}, u32[]{:S(2)}) copy-start(s32[384]{0:T(512)} %param.5) | copy-start | bytes 4612
  14.9 21.3 %collective-permute-start = (bf16[8,2,2,16,769]{4,3,2,1,0:T(8,128)(2,1)S(1)}, bf16[8,2,2,16,769]{4,3,2,1,0:T(8,128)(2,1)S(1)}, u32[]{:S(2)}, u32[]{:S(2)}) collective-permute-start(bf16[8,2,2,16,769]{4,3,2,1,0:T(8,128)(2,1)S(1)} %get-tuple-element.12), channel_id=1, source_target_pairs={{0,1},{1,0},{2,3},{3,2},{4,5},{5,4},{6,7},{7,6},{8,9},{9,8},{10,11... | collective-permute-start | bytes 2362376 | tf_op jit(solution)/shard_map/ppermute | solution.py:264
  36.2 0.9 copy-start.6
  59.3 60.4 %all-to-all-start = ((bf16[16,2,2,16,1152]{4,3,2,1,0:T(8,128)(2,1)}), bf16[16,2,2,16,1152]{4,3,2,1,0:T(8,128)(2,1)S(1)}, u32[]{:S(2)}, u32[]{:S(2)}) async-start(bf16[16,2,2,16,1152]{4,3,2,1,0:T(8,128)(2,1)} %pack.4), calls=%async_computation | async-start | bytes 4718592 | tf_op jit(solution)/shard_map/all_to_all | solution.py:258
  66.7 21.5 %collective-permute-start.2 = (bf16[8,2,2,16,769]{4,3,2,1,0:T(8,128)(2,1)S(1)}, bf16[8,2,2,16,769]{4,3,2,1,0:T(8,128)(2,1)S(1)}, u32[]{:S(2)}, u32[]{:S(2)}) collective-permute-start(bf16[8,2,2,16,769]{4,3,2,1,0:T(8,128)(2,1)S(1)} %get-tuple-element.11), channel_id=1, source_target_pairs={{0,1},{1,0},{2,3},{3,2},{4,5},{5,4},{6,7},{7,6},{8,9},{9,8},{10,11... | collective-permute-start | bytes 2362376 | tf_op jit(solution)/shard_map/ppermute | solution.py:264
  88.2 1.0 copy-start.7
  119.7 33.7 %copy-start.1 = (bf16[16,2,2,16,1152]{4,3,2,1,0:T(8,128)(2,1)}, bf16[16,2,2,16,1152]{4,3,2,1,0:T(8,128)(2,1)S(1)}, u32[]{:S(2)}) copy-start(bf16[16,2,2,16,1152]{4,3,2,1,0:T(8,128)(2,1)S(1)} %all-to-all-done.refs_0_) | copy-start | bytes 7077892
  119.7 116.7 %all-to-all-start.3 = ((bf16[16,2,2,16,1152]{4,3,2,1,0:T(8,128)(2,1)}), bf16[16,2,2,16,1152]{4,3,2,1,0:T(8,128)(2,1)}, u32[]{:S(2)}, u32[]{:S(2)}) async-start(bf16[16,2,2,16,1152]{4,3,2,1,0:T(8,128)(2,1)} %pack.6), calls=%async_computation.3 | async-start | bytes 4718592 | tf_op jit(solution)/shard_map/all_to_all | solution.py:258
  157.0 41.2 %collective-permute-start.1 = (bf16[16,2,2,16,769]{4,3,2,1,0:T(8,128)(2,1)S(1)}, bf16[16,2,2,16,769]{4,3,2,1,0:T(8,128)(2,1)S(1)}, u32[]{:S(2)}, u32[]{:S(2)}) collective-permute-start(bf16[16,2,2,16,769]{4,3,2,1,0:T(8,128)(2,1)S(1)} %get-tuple-element.10), channel_id=1, source_target_pairs={{0,1},{1,0},{2,3},{3,2},{4,5},{5,4},{6,7},{7,6},{8,9},{9,8},{10,11... | collective-permute-start | bytes 4724744 | tf_op jit(solution)/shard_map/ppermute | solution.py:264
  198.2 1.2 copy-start.5
  236.4 86.4 %all-to-all-start.2 = ((bf16[16,1,2,32,1152]{4,3,2,1,0:T(8,128)(2,1)}), bf16[16,1,2,32,1152]{4,3,2,1,0:T(8,128)(2,1)S(1)}, u32[]{:S(2)}, u32[]{:S(2)}) async-start(bf16[16,1,2,32,1152]{4,3,2,1,0:T(8,128)(2,1)} %get-tuple-element.8), calls=%async_computation.2 | async-start | bytes 4718592 | tf_op jit(solution)/shard_map/all_to_all | solution.py:258
  243.3 41.4 %collective-permute-start.3 = (bf16[16,2,2,16,769]{4,3,2,1,0:T(8,128)(2,1)}, bf16[16,2,2,16,769]{4,3,2,1,0:T(8,128)(2,1)S(1)}, u32[]{:S(2)}, u32[]{:S(2)}) collective-permute-start(bf16[16,2,2,16,769]{4,3,2,1,0:T(8,128)(2,1)} %get-tuple-element.9), channel_id=1, source_target_pairs={{0,1},{1,0},{2,3},{3,2},{4,5},{5,4},{6,7},{7,6},{8,9},{9,8},{10,11... | collective-permute-start | bytes 4724744 | tf_op jit(solution)/shard_map/ppermute | solution.py:264
  284.7 1.3 copy-start.4
  322.8 110.4 %copy-start.2 = (bf16[16,1,2,32,1152]{4,3,2,1,0:T(8,128)(2,1)}, bf16[16,1,2,32,1152]{4,3,2,1,0:T(8,128)(2,1)S(1)}, u32[]{:S(2)}) copy-start(bf16[16,1,2,32,1152]{4,3,2,1,0:T(8,128)(2,1)S(1)} %all-to-all-done.2.refs_1_) | copy-start | bytes 7077892
  433.2 64.8 %all-to-all-start.1 = ((bf16[16,1,2,32,1152]{4,3,2,1,0:T(8,128)(2,1)}), bf16[16,1,2,32,1152]{4,3,2,1,0:T(8,128)(2,1)S(1)}, u32[]{:S(2)}, u32[]{:S(2)}) async-start(bf16[16,1,2,32,1152]{4,3,2,1,0:T(8,128)(2,1)} %get-tuple-element.7), calls=%async_computation.1 | async-start | bytes 4718592 | tf_op jit(solution)/shard_map/all_to_all | solution.py:258
  498.1 1.5 copy-start.3
